TPU v7x, 32 devices: a whole 2x2x4 slice. The times are simulated.
32 devices in a mesh: tok: 8 (over z, y), voc: 4 (over x, core).
Axes of the slice: x: 2, y: 2, z: 4, core: 2. Of those that a mesh axis runs over, the one named last changes fastest.
Arguments:
- hidden: bfloat16 [1024, 3584], P('tok', 'voc'), may hold values from -36 to 36
- weight: bfloat16 [3584, 256000], P(None, ('voc', 'tok')), may hold values from -1 to 1
- targets: int32 [1024], replicated, may hold values from 0 to 255999
- slot: int32 [8], replicated, may hold values from 0 to 7, each once
- prompt_len: int32 [8], replicated, may hold values from 1 to 64
- ref_means: float32 [8], replicated, may hold values from -17 to -13
Outputs:
- token_logprobs: float32 [1024], P('tok')
- margins: float32 [4], replicated
- loss: float32 [], replicated
All inputs are finite; a program needn't handle non-finite values.
Results may differ from a plain program's by a relative error of at most 0.0003.
Values may be sent and summed in bfloat16 or wider, within the bound.
A program may use at most 192 MiB of HBM per device.

v0:
```python
import functools

import jax
import jax.numpy as jnp
from jax import lax
from jax.experimental import pallas as pl
from jax.experimental.pallas import tpu as pltpu
from jax.sharding import PartitionSpec as P

beta_scale = 2.0
LOW = -1e30
LANES = 128
TILE = 512
CHUNK = 64
NT = (((1,), (1,)), ((), ()))


def stats_pass(x_ref, tgt_ref, m_ref, s_ref, t_ref, base, cols):
    lane = lax.broadcasted_iota(jnp.int32, (CHUNK, LANES), 1)
    for r in range(0, x_ref.shape[0], CHUNK):
        rows = pl.ds(r, CHUNK)
        wanted = tgt_ref[rows, :] - base
        xs = []
        for k in range(TILE // LANES):
            x = x_ref[rows, k * LANES : (k + 1) * LANES]
            xs.append(jnp.where(lane < cols - base - k * LANES, x, LOW))
        m_old = m_ref[rows, :]
        m_new = functools.reduce(jnp.maximum, xs, m_old)
        s = s_ref[rows, :] * jnp.exp(m_old - m_new)
        t = t_ref[rows, :]
        for k, x in enumerate(xs):
            s = s + jnp.exp(x - m_new)
            t = t + jnp.where(wanted == lane + k * LANES, x, 0.0)
        m_ref[rows, :] = m_new
        s_ref[rows, :] = s
        t_ref[rows, :] = t


def logits_kernel(cols, h_ref, w_ref, tgt_ref, out_ref, a_ref, b_ref, m_ref, s_ref, t_ref):
    step = pl.program_id(0)

    @pl.when(step == 0)
    def _():
        b_ref[...] = jnp.full_like(b_ref, LOW)
        m_ref[...] = jnp.full_like(m_ref, LOW)
        s_ref[...] = jnp.zeros_like(s_ref)
        t_ref[...] = jnp.zeros_like(t_ref)

    base = step * (2 * TILE)
    fold = functools.partial(stats_pass, tgt_ref=tgt_ref, m_ref=m_ref, s_ref=s_ref, t_ref=t_ref, cols=cols)
    a_ref[...] = lax.dot_general(h_ref[...], w_ref[:TILE], NT, preferred_element_type=jnp.float32)
    fold(b_ref, base=base - TILE)
    b_ref[...] = lax.dot_general(h_ref[...], w_ref[TILE:], NT, preferred_element_type=jnp.float32)
    fold(a_ref, base=base)

    @pl.when(step == pl.num_programs(0) - 1)
    def _():
        fold(b_ref, base=base + TILE)
        diagonal = lax.broadcasted_iota(jnp.int32, (LANES, LANES), 0) == lax.broadcasted_iota(jnp.int32, (LANES, LANES), 1)
        for q in range(out_ref.shape[1]):
            rows = pl.ds(q * LANES, LANES)
            m = m_ref[rows, :]
            top = jnp.max(m, axis=1, keepdims=True)
            total = jnp.sum(s_ref[rows, :] * jnp.exp(m - top), axis=1, keepdims=True)
            lse = top + jnp.log(total)
            hit = jnp.sum(t_ref[rows, :], axis=1, keepdims=True)
            out_ref[0, pl.ds(q, 1), :] = jnp.sum(jnp.where(diagonal, lse, 0.0), axis=0, keepdims=True)
            out_ref[1, pl.ds(q, 1), :] = jnp.sum(jnp.where(diagonal, hit, 0.0), axis=0, keepdims=True)


def local_stats(full, weight, wanted):
    rows, depth = full.shape
    cols = weight.shape[0]
    steps = pl.cdiv(cols, 2 * TILE)
    whole = lambda i: (0, 0)
    return pl.pallas_call(
        functools.partial(logits_kernel, cols),
        grid=(steps,),
        out_shape=jax.ShapeDtypeStruct((2, rows // LANES, LANES), jnp.float32),
        in_specs=[
            pl.BlockSpec((rows, depth), whole),
            pl.BlockSpec((2 * TILE, depth), lambda i: (i, 0)),
            pl.BlockSpec((rows, LANES), whole),
        ],
        out_specs=pl.BlockSpec((2, rows // LANES, LANES), lambda i: (0, 0, 0)),
        scratch_shapes=[pltpu.VMEM((rows, TILE), jnp.float32)] * 2 + [pltpu.VMEM((rows, LANES), jnp.float32)] * 3,
        compiler_params=pltpu.CompilerParams(vmem_limit_bytes=62 * 1024 * 1024, dimension_semantics=("arbitrary",)),
        cost_estimate=pl.CostEstimate(flops=2 * rows * depth * cols, bytes_accessed=2 * depth * (rows + cols), transcendentals=rows * cols),
    )(full, weight, wanted)


def finish_kernel(n_tok, n_dev, stats_ref, slot_ref, prompt_ref, ref_ref, own_ref, margin_ref, loss_ref, got, send_sem, recv_sem):
    me = lax.axis_index("voc") * n_tok + lax.axis_index("tok")

    def peer(k):
        other = lax.rem(me + k, n_dev)
        return {"tok": lax.rem(other, n_tok), "voc": lax.div(other, n_tok)}

    barrier = pltpu.get_barrier_semaphore()

    @pl.loop(1, n_dev)
    def _(k):
        pl.semaphore_signal(barrier, inc=1, device_id=peer(k), device_id_type=pl.DeviceIdType.MESH)

    pl.semaphore_wait(barrier, n_dev - 1)

    def copy(k, source):
        return pltpu.make_async_remote_copy(
            src_ref=stats_ref,
            dst_ref=got.at[source],
            send_sem=send_sem.at[k],
            recv_sem=recv_sem.at[k],
            device_id=peer(k),
            device_id_type=pl.DeviceIdType.MESH,
        )

    keep = pltpu.make_async_copy(stats_ref, got.at[me], send_sem.at[0])
    keep.start()

    @pl.loop(1, n_dev)
    def _(k):
        copy(k, me).start()

    @pl.loop(1, n_dev)
    def _(k):
        copy(k, lax.rem(me + n_dev - k, n_dev)).wait_recv()

    @pl.loop(1, n_dev)
    def _(k):
        copy(k, me).wait_send()

    keep.wait()
    top = got[0, 0]
    target = got[0, 1]
    for k in range(1, n_dev):
        top = jnp.maximum(top, got[k, 0])
        target = target + got[k, 1]
    total = jnp.zeros_like(top)
    for k in range(n_dev):
        total = total + jnp.exp(got[k, 0] - top)
    token_lp = target - (top + jnp.log(total))
    seqs, width = token_lp.shape
    row = lax.broadcasted_iota(jnp.int32, (seqs, width), 0)
    lane = lax.broadcasted_iota(jnp.int32, (seqs, width), 1)
    mine = row == lax.axis_index("tok")
    own_ref[...] = jnp.sum(jnp.where(mine, token_lp, 0.0), axis=0, keepdims=True)
    prompt = prompt_ref[...]
    reply = jnp.sum(jnp.where(lane >= prompt, token_lp, 0.0), axis=1, keepdims=True)
    advantage = reply / (width - prompt[:, :1]).astype(jnp.float32) - ref_ref[:, :1]
    slot = slot_ref[...]
    chosen = lax.bitwise_and(slot, 1) == 0
    signed = jnp.where(chosen, advantage, -advantage)
    pair = lax.shift_right_logical(slot, 1)
    margins = beta_scale * jnp.sum(jnp.where(pair == lane, signed, 0.0), axis=0, keepdims=True)
    margin_ref[...] = margins
    softplus = jnp.maximum(-margins, 0.0) + jnp.log1p(jnp.exp(-jnp.abs(margins)))
    n_pairs = seqs // 2
    loss = jnp.sum(jnp.where(lane[:1] < n_pairs, softplus, 0.0), axis=1, keepdims=True) / n_pairs
    loss_ref[...] = jnp.broadcast_to(loss, loss_ref.shape)


def exchange_and_finish(stats, slot, prompt_len, ref_means):
    n_tok = lax.axis_size("tok")
    n_dev = n_tok * lax.axis_size("voc")
    seqs, width = stats.shape[1:]
    wide = lambda v: jnp.broadcast_to(v[:, None], (seqs, width))
    row = jax.ShapeDtypeStruct((1, width), jnp.float32)
    own, margins, loss = pl.pallas_call(
        functools.partial(finish_kernel, n_tok, n_dev),
        out_shape=(row, row, row),
        in_specs=[pl.BlockSpec(memory_space=pltpu.VMEM)] * 4,
        out_specs=(pl.BlockSpec(memory_space=pltpu.VMEM),) * 3,
        scratch_shapes=[
            pltpu.VMEM((n_dev,) + stats.shape, jnp.float32),
            pltpu.SemaphoreType.DMA((n_dev,)),
            pltpu.SemaphoreType.DMA((n_dev,)),
        ],
        compiler_params=pltpu.CompilerParams(collective_id=1, has_side_effects=True),
    )(stats, wide(slot), wide(prompt_len), wide(ref_means))
    return own.reshape(-1), margins[0, : seqs // 2], loss[0, 0]


def gather_kernel(n_tok, hidden_ref, full_ref, local_sem, send_sem, recv_sem):
    tok, voc = lax.axis_index("tok"), lax.axis_index("voc")
    rows, width = hidden_ref.shape
    half = rows // 2
    n_z = n_tok // 2
    z, y = tok // 2, tok % 2
    other_y = tok + 1 - 2 * y
    other_x = (voc + 2) % 4
    sibling = voc + 1 - 2 * (voc % 2)
    to_x = {"tok": tok, "voc": other_x}
    to_y = {"tok": other_y, "voc": voc}
    to_sibling = {"tok": tok, "voc": sibling}

    def tok_at(offset, row):
        return ((z + offset) % n_z) * 2 + row

    barrier = pltpu.get_barrier_semaphore()
    for offset in range(1, n_z):
        pl.semaphore_signal(barrier, inc=1, device_id={"tok": tok_at(offset, y), "voc": voc}, device_id_type=pl.DeviceIdType.MESH)
    for peer in (to_x, to_y, to_sibling):
        pl.semaphore_signal(barrier, inc=1, device_id=peer, device_id_type=pl.DeviceIdType.MESH)
    pl.semaphore_wait(barrier, n_z + 2)

    def place(t, v, first=0, count=rows):
        return full_ref.at[pl.ds(pl.multiple_of(t * rows + first, 32), count), pl.ds(pl.multiple_of(v * width, LANES), width)]

    Z, X, Y, XH, YH, SZ, SX, SY, SXH, SYH = range(10)
    sent = []

    def send(kind, offset, source, target, device):
        index = kind * n_z + offset
        copy = pltpu.make_async_remote_copy(
            src_ref=source,
            dst_ref=target,
            send_sem=send_sem.at[index],
            recv_sem=recv_sem.at[index],
            device_id=device,
            device_id_type=pl.DeviceIdType.MESH,
        )
        copy.start()
        sent.append(copy)

    def arrived(kind, offset, target):
        index = kind * n_z + offset
        pltpu.make_async_remote_copy(
            src_ref=target,
            dst_ref=target,
            send_sem=send_sem.at[index],
            recv_sem=recv_sem.at[index],
            device_id=to_sibling,
            device_id_type=pl.DeviceIdType.MESH,
        ).wait_recv()

    own = place(tok, voc)
    for offset in sorted(range(1, n_z), key=lambda o: min(o, n_z - o)):
        send(Z, offset, hidden_ref, own, {"tok": tok_at(n_z - offset, y), "voc": voc})

    def spread(offset, source):
        here = place(tok_at(offset, y), voc)
        send(X, offset, source, here, to_x)
        send(Y, offset, source, here, to_y)
        send(SZ, offset, source, here, to_sibling)

    def forward(offset):
        across_x = (tok_at(offset, y), other_x)
        arrived(X, offset, place(*across_x))
        part = place(*across_x, 0, half)
        send(YH, offset, part, part, to_y)
        send(SX, offset, place(*across_x), place(*across_x), to_sibling)
        across_y = (tok_at(offset, 1 - y), voc)
        arrived(Y, offset, place(*across_y))
        part = place(*across_y, half, half)
        send(XH, offset, part, part, to_x)
        send(SY, offset, place(*across_y), place(*across_y), to_sibling)

    def finish(offset):
        corner = (tok_at(offset, 1 - y), other_x)
        for kind, sib, first in ((YH, SYH, 0), (XH, SXH, half)):
            part = place(*corner, first, half)
            arrived(kind, offset, part)
            send(sib, offset, part, part, to_sibling)

    order = sorted(range(n_z), key=lambda o: min(o, n_z - o))
    for i in range(n_z + 2):
        if i == 0:
            spread(0, hidden_ref)
            keep = pltpu.make_async_copy(hidden_ref, own, local_sem)
            keep.start()
        elif i < n_z:
            here = place(tok_at(order[i], y), voc)
            arrived(Z, order[i], here)
            spread(order[i], here)
        if 1 <= i <= n_z:
            forward(order[i - 1])
        if i >= 2:
            finish(order[i - 2])
    far_x = other_x + 1 - 2 * (other_x % 2)
    for o in range(n_z):
        arrived(SZ, o, place(tok_at(o, y), sibling))
        arrived(SX, o, place(tok_at(o, y), far_x))
        arrived(SY, o, place(tok_at(o, 1 - y), sibling))
        arrived(SYH, o, place(tok_at(o, 1 - y), far_x, 0, half))
        arrived(SXH, o, place(tok_at(o, 1 - y), far_x, half, half))
    keep.wait()
    for copy in sent:
        copy.wait_send()


def gather_hidden(hidden):
    n_tok, n_voc = lax.axis_size("tok"), lax.axis_size("voc")
    rows, width = hidden.shape
    if n_voc != 4 or n_tok % 2 or width % LANES or rows % 64:
        all_rows = lax.all_gather(hidden, "tok", axis=0, tiled=True)
        return lax.all_gather(all_rows, "voc", axis=1, tiled=True)
    copies = 10 * (n_tok // 2)
    return pl.pallas_call(
        functools.partial(gather_kernel, n_tok),
        out_shape=jax.ShapeDtypeStruct((rows * n_tok, width * n_voc), hidden.dtype),
        in_specs=[pl.BlockSpec(memory_space=pl.ANY)],
        out_specs=pl.BlockSpec(memory_space=pl.ANY),
        scratch_shapes=[
            pltpu.SemaphoreType.DMA,
            pltpu.SemaphoreType.DMA((copies,)),
            pltpu.SemaphoreType.DMA((copies,)),
        ],
        compiler_params=pltpu.CompilerParams(collective_id=2, has_side_effects=True),
    )(hidden)


def body(hidden, weight, targets, slot, prompt_len, ref_means):
    vocab_cols = weight.shape[1]
    col_start = (lax.axis_index("voc") * lax.axis_size("tok") + lax.axis_index("tok")) * vocab_cols
    local = targets - col_start
    local = jnp.where((local >= 0) & (local < vocab_cols), local, -(1 << 30))
    wanted = jnp.broadcast_to(local[:, None], (targets.shape[0], LANES))
    stats = local_stats(gather_hidden(hidden), weight.T, wanted)
    return exchange_and_finish(stats, slot, prompt_len, ref_means)


def solution(mesh):
    in_specs = (P("tok", "voc"), P(None, ("voc", "tok")), P(), P(), P(), P())
    out_specs = (P("tok"), P(), P())
    return jax.shard_map(body, mesh=mesh, in_specs=in_specs, out_specs=out_specs, check_vma=False)
```

profile of v0, /device:TPU:0, one launch (start us, length us, event | category | flops | bytes accessed | tf_op | source)
XLA Modules:
  0.0 135.5 jit_solution(12224409587072094529)
XLA Ops:
  0.6 0.7 and_select_fusion
  1.3 1.0 broadcast_in_dim.13.tgt_ref
  2.3 43.5 %shard_map.85.h_ref = bf16[1024,3584]{1,0:T(8,128)(2,1)} custom-call(bf16[128,896]{1,0:T(8,128)(2,1)} %hidden_ref.1), custom_call_target="tpu_custom_call" | custom-call | tf_op jit(solution)/shard_map/pallas_call | solution.py:298
  45.8 0.0 copy-start
  45.8 0.0 copy-start.1
  45.9 0.0 copy-start.2
  45.9 70.0 %shard_map.86.stats_ref = f32[2,8,128]{2,1,0:T(8,128)} custom-call(bf16[1024,3584]{1,0:T(8,128)(2,1)} %shard_map.85.h_ref, bf16[8000,3584]{1,0:T(8,128)(2,1)} %bitcast.6, s32[1024,128]{1,0:T(8,128)} %broadcast_in_dim.13.tgt_ref), custom_call_target="tpu_custom_call" | custom-call | flops 58720256000 | bytes 64684032 | tf_op jit(solution)/shard_map/pallas_call | solution.py:76
  115.9 0.0 copy-done
  115.9 0.7 broadcast_in_dim.14.slot_ref
  116.5 0.0 copy-done.1
  116.5 0.7 broadcast_in_dim.15.prompt_ref
  117.2 0.0 copy-done.2
  117.2 0.7 broadcast_in_dim.16.ref_ref
  117.9 13.5 %shard_map.87 = (f32[1,128]{1,0:T(1,128)}, f32[1,128]{1,0:T(1,128)}, f32[1,128]{1,0:T(1,128)}) custom-call(f32[2,8,128]{2,1,0:T(8,128)} %shard_map.86.stats_ref, s32[8,128]{1,0:T(8,128)} %broadcast_in_dim.14.slot_ref, s32[8,128]{1,0:T(8,128)} %broadcast_in_dim.15.prompt_ref, f32[8,128]{1,0:T(8,128)} %broadcast_in_dim.16.ref_ref), custom_call_target="tpu_custom_call" | custom-call | tf_op jit(solution)/shard_map/pallas_call | solution.py:168
  131.4 1.1 slice_bitcast_fusion
  132.5 1.2 copy.11
Async XLA Ops:
  45.8 70.0 %copy-start = (s32[8]{0:T(128)S(1)}, s32[8]{0:T(128)}, u32[]{:S(2)}) copy-start(s32[8]{0:T(128)} %param.9) | copy-start | bytes 100
  45.8 70.7 %copy-start.1 = (s32[8]{0:T(128)S(1)}, s32[8]{0:T(128)}, u32[]{:S(2)}) copy-start(s32[8]{0:T(128)} %param.10) | copy-start | bytes 100
  45.9 71.3 %copy-start.2 = (f32[8]{0:T(128)S(1)}, f32[8]{0:T(128)}, u32[]{:S(2)}) copy-start(f32[8]{0:T(128)} %param.11) | copy-start | bytes 100
where the time goes:
time: 136 us
  Pallas kernels  127 us (93%)
  local copies, waits for them, and re-layouts  5.28 us (4%)
  between operations  2.49 us (2%)
    pallas_call x1, Pallas kernels, local_stats(): pl.pallas_call(functools.partial(logits_kernel, cols), grid=(steps,), out...  70 us
    pallas_call x1, Pallas kernels, gather_hidden(): pl.pallas_call(functools.partial(gather_kernel, n_tok), out_shape=jax.Sha...  43.5 us
    pallas_call x1, Pallas kernels, exchange_and_finish(): pl.pallas_call(functools.partial(finish_kernel, n_tok, n_dev), out_shape=...  13.5 us

commit v1 on v0

--- a/solution.py
+++ b/solution.py
@@ -10,6 +10,7 @@
 beta_scale = 2.0
 LOW = -1e30
 LANES = 128
+SUBS = 8
 TILE = 512
 CHUNK = 64
 NT = (((1,), (1,)), ((), ()))
@@ -309,8 +310,338 @@
     )(hidden)
 
 
+def plan_rows(cols):
+    fits = [t for t in range(16, 801, 16) if cols % (2 * t) == 0]
+    return fits[-1] if fits else 0
+
+
+def fold_tile(x_ref, wanted, base, m_ref, s_ref, t_ref):
+    rows, width = x_ref.shape
+    lanes = 4
+    sub = lax.broadcasted_iota(jnp.int32, (SUBS, LANES), 0)
+    for c in range(width // LANES):
+        at = slice(c * LANES, (c + 1) * LANES)
+        m_old = m_ref[:, at]
+        tops = [m_old] + [jnp.full_like(m_old, LOW)] * (lanes - 1)
+        for i in range(rows // SUBS):
+            tops[i % lanes] = jnp.maximum(tops[i % lanes], x_ref[i * SUBS : (i + 1) * SUBS, at])
+        m_new = functools.reduce(jnp.maximum, tops)
+        sums = [s_ref[:, at] * jnp.exp(m_old - m_new)] + [jnp.zeros_like(m_old)] * (lanes - 1)
+        hits = [t_ref[:, at]] + [jnp.zeros_like(m_old)] * (lanes - 1)
+        want = wanted[c] - base - sub
+        for i in range(rows // SUBS):
+            x = x_ref[i * SUBS : (i + 1) * SUBS, at]
+            sums[i % lanes] = sums[i % lanes] + jnp.exp(x - m_new)
+            hits[i % lanes] = hits[i % lanes] + jnp.where(want == i * SUBS, x, 0.0)
+        m_ref[:, at] = m_new
+        s_ref[:, at] = functools.reduce(jnp.add, sums)
+        t_ref[:, at] = functools.reduce(jnp.add, hits)
+
+
+def fused_kernel(
+    n_tok, n_dev, tile,
+    hidden_ref, weight_ref, tgt_ref, slot_ref, prompt_ref, ref_ref, out_ref,
+    full_ref, ring_ref, a_ref, b_ref, m_ref, s_ref, t_ref, got_ref, lp_ref,
+    ring_sem, local_sem, send_sem, recv_sem, stat_send, stat_recv,
+):
+    tok, voc = lax.axis_index("tok"), lax.axis_index("voc")
+    me = voc * n_tok + tok
+    rows, width = hidden_ref.shape
+    cols = weight_ref.shape[0]
+    half = rows // 2
+    n_z = n_tok // 2
+    z, y = tok // 2, tok % 2
+    other_y = tok + 1 - 2 * y
+    other_x = (voc + 2) % 4
+    sibling = voc + 1 - 2 * (voc % 2)
+    far_x = other_x + 1 - 2 * (other_x % 2)
+    to_x = {"tok": tok, "voc": other_x}
+    to_y = {"tok": other_y, "voc": voc}
+    to_sibling = {"tok": tok, "voc": sibling}
+
+    pairs = cols // (2 * tile)
+    slots = ring_ref.shape[0]
+    sweeps = 3
+
+    def load(n, part):
+        start = pl.multiple_of((lax.rem(n, pairs) * 2 + part) * tile, 16)
+        return pltpu.make_async_copy(
+            weight_ref.at[pl.ds(start, tile)],
+            ring_ref.at[lax.rem(n, slots), pl.ds(part * tile, tile)],
+            ring_sem.at[lax.rem(n, slots), part],
+        )
+
+    def place(o, t, v, first=0, count=rows):
+        return full_ref.at[pl.ds(pl.multiple_of((2 * o + t) * rows + first, 32), count), pl.ds(pl.multiple_of(v * width, LANES), width)]
+
+    keep = pltpu.make_async_copy(hidden_ref, place(0, y, voc), local_sem)
+    keep.start()
+    for n in range(slots):
+        for part in range(2):
+            load(n, part).start()
+
+    def peer(k):
+        other = lax.rem(me + k, n_dev)
+        return {"tok": lax.rem(other, n_tok), "voc": lax.div(other, n_tok)}
+
+    barrier = pltpu.get_barrier_semaphore()
+
+    @pl.loop(1, n_dev)
+    def _(k):
+        pl.semaphore_signal(barrier, inc=1, device_id=peer(k), device_id_type=pl.DeviceIdType.MESH)
+
+    keep.wait()
+    pl.semaphore_wait(barrier, n_dev - 1)
+
+    Z, X, Y, XH, YH, SZ, SX, SY, SXH, SYH = range(10)
+    sent = []
+
+    def copy(kind, o):
+        t, v, first, count, device = {
+            Z: (y, voc, 0, rows, {"tok": ((z + n_z - o) % n_z) * 2 + y, "voc": voc}),
+            X: (y, voc, 0, rows, to_x),
+            Y: (y, voc, 0, rows, to_y),
+            SZ: (y, voc, 0, rows, to_sibling),
+            YH: (y, other_x, 0, half, to_y),
+            SX: (y, other_x, 0, rows, to_sibling),
+            XH: (1 - y, voc, half, half, to_x),
+            SY: (1 - y, voc, 0, rows, to_sibling),
+            SYH: (1 - y, other_x, 0, half, to_sibling),
+            SXH: (1 - y, other_x, half, half, to_sibling),
+        }[kind]
+        source = place(0 if kind == Z else o, t, v, first, count)
+        return pltpu.make_async_remote_copy(
+            src_ref=source,
+            dst_ref=place(o, t, v, first, count),
+            send_sem=send_sem.at[kind * n_z + o],
+            recv_sem=recv_sem.at[kind * n_z + o],
+            device_id=device,
+            device_id_type=pl.DeviceIdType.MESH,
+        )
+
+    def send(kind, o):
+        copy(kind, o).start()
+        sent.append((kind, o))
+
+    def arrived(kind, o):
+        t, v, first, count = {
+            Z: (y, voc, 0, rows),
+            X: (y, other_x, 0, rows),
+            Y: (1 - y, voc, 0, rows),
+            SZ: (y, sibling, 0, rows),
+            YH: (1 - y, other_x, 0, half),
+            SX: (y, far_x, 0, rows),
+            XH: (1 - y, other_x, half, half),
+            SY: (1 - y, sibling, 0, rows),
+            SYH: (1 - y, far_x, 0, half),
+            SXH: (1 - y, far_x, half, half),
+        }[kind]
+        target = place(o, t, v, first, count)
+        pltpu.make_async_remote_copy(
+            src_ref=target,
+            dst_ref=target,
+            send_sem=send_sem.at[kind * n_z + o],
+            recv_sem=recv_sem.at[kind * n_z + o],
+            device_id=to_sibling,
+            device_id_type=pl.DeviceIdType.MESH,
+        ).wait_recv()
+
+    def spread(o):
+        if o:
+            arrived(Z, o)
+        for kind in (X, Y, SZ):
+            send(kind, o)
+
+    def forward(o):
+        arrived(X, o)
+        send(YH, o)
+        send(SX, o)
+        arrived(Y, o)
+        send(XH, o)
+        send(SY, o)
+
+    def finish(o):
+        arrived(YH, o)
+        send(SYH, o)
+        arrived(XH, o)
+        send(SXH, o)
+
+    def settle(o):
+        for kind in (SZ, SX, SY, SYH, SXH):
+            arrived(kind, o)
+
+    def stat_copy(k, source, piece):
+        part = got_ref.at[source, pl.ds(piece * 2, 2)]
+        return pltpu.make_async_remote_copy(
+            src_ref=part,
+            dst_ref=part,
+            send_sem=stat_send.at[piece, k],
+            recv_sem=stat_recv.at[piece, k],
+            device_id=peer(k),
+            device_id_type=pl.DeviceIdType.MESH,
+        )
+
+    def tell(piece):
+        @pl.loop(1, n_dev)
+        def _(k):
+            stat_copy(k, me, piece).start()
+
+    spread(0)
+    for o in (1, 3, 2):
+        send(Z, o)
+    forward(0)
+    finish(0)
+    settle(0)
+
+    col_start = me * cols
+
+    def sweep(turn, first, planes, actions):
+        size = planes * 2 * rows
+        wanted = []
+        for o in range(first, first + planes):
+            for t in range(2):
+                local = tgt_ref[pl.ds(((z + o) % n_z) * 2 + t, 1), :] - col_start
+                wanted.append(jnp.where((local >= 0) & (local < cols), local, -(1 << 30)))
+        x_a, x_b = a_ref.at[:, pl.ds(0, size)], b_ref.at[:, pl.ds(0, size)]
+        m, s, t = (r.at[:, pl.ds(0, size)] for r in (m_ref, s_ref, t_ref))
+        x_b[...] = jnp.full_like(x_b, LOW)
+        m[...] = jnp.full_like(m, LOW)
+        s[...] = jnp.zeros_like(s)
+        t[...] = jnp.zeros_like(t)
+
+        def step(i, carry):
+            n = turn * pairs + i
+            for at, action in actions:
+                pl.when(i == at)(action)
+            for part in range(2):
+                load(n, part).wait()
+
+            @pl.when((n >= 1) & (n - 1 + slots < sweeps * pairs))
+            def _():
+                for part in range(2):
+                    load(n - 1 + slots, part).start()
+
+            slot = lax.rem(n, slots)
+            h = lambda: full_ref[first * 2 * rows : first * 2 * rows + size, :]
+            base = i * (2 * tile)
+            x_a[...] = lax.dot_general(ring_ref[slot, :tile, :], h(), NT, preferred_element_type=jnp.float32)
+            fold_tile(x_b, wanted, base - tile, m, s, t)
+            x_b[...] = lax.dot_general(ring_ref[slot, tile:, :], h(), NT, preferred_element_type=jnp.float32)
+            fold_tile(x_a, wanted, base, m, s, t)
+            return carry
+
+        lax.fori_loop(0, pairs, step, 0)
+        fold_tile(x_b, wanted, cols - tile, m, s, t)
+        high = m[...]
+        top = jnp.max(high, axis=0, keepdims=True)
+        total = jnp.sum(s[...] * jnp.exp(high - top), axis=0, keepdims=True)
+        lse = top + jnp.log(total)
+        hit = jnp.sum(t[...], axis=0, keepdims=True)
+        for p in range(planes):
+            for q in range(2):
+                at = slice((2 * p + q) * LANES, (2 * p + q + 1) * LANES)
+                got_ref[me, first + p, q : q + 1, :] = lse[:, at]
+                got_ref[me, first + p, 2 + q : 3 + q, :] = hit[:, at]
+
+    def act(*calls):
+        def run():
+            for call, o in calls:
+                call(o)
+
+        return run
+
+    sweep(0, 0, 1, [(0, act((spread, 1))), (2, act((forward, 1), (spread, 3))), (4, act((finish, 1), (forward, 3), (spread, 2)))])
+    settle(1)
+    sweep(1, 1, 1, [(1, act((finish, 3), (forward, 2))), (3, act((finish, 2)))])
+    settle(3)
+    settle(2)
+    sweep(2, 2, 2, [(1, act((tell, 0)))])
+    tell(1)
+    for kind, o in sent:
+        copy(kind, o).wait_send()
+
+    @pl.loop(1, n_dev)
+    def _(k):
+        for piece in range(2):
+            stat_copy(k, lax.rem(me + n_dev - k, n_dev), piece).wait_recv()
+
+    @pl.loop(1, n_dev)
+    def _(k):
+        for piece in range(2):
+            stat_copy(k, me, piece).wait_send()
+
+    for g in range(n_z):
+        of = lambda k: got_ref[k, (g - (k % n_tok) // 2) % n_z]
+        top = functools.reduce(jnp.maximum, [of(k)[:2] for k in range(n_dev)])
+        total = functools.reduce(jnp.add, [jnp.exp(of(k)[:2] - top) for k in range(n_dev)])
+        hit = functools.reduce(jnp.add, [of(k)[2:] for k in range(n_dev)])
+        lp_ref[2 * g : 2 * g + 2, :] = hit - (top + jnp.log(total))
+    token_lp = lp_ref[...]
+    seqs, length = token_lp.shape
+    row = lax.broadcasted_iota(jnp.int32, (seqs, length), 0)
+    lane = lax.broadcasted_iota(jnp.int32, (seqs, length), 1)
+    spread_out = lambda ref: functools.reduce(lambda v, q: jnp.where(row == q, ref[q], v), range(1, seqs), jnp.full(row.shape, ref[0]))
+    prompt, slot, ref_mean = spread_out(prompt_ref), spread_out(slot_ref), spread_out(ref_ref)
+    own = jnp.sum(jnp.where(row == tok, token_lp, 0.0), axis=0, keepdims=True)
+    reply = jnp.sum(jnp.where(lane >= prompt, token_lp, 0.0), axis=1, keepdims=True)
+    advantage = reply / (length - prompt).astype(jnp.float32) - ref_mean
+    signed = jnp.where(lax.bitwise_and(slot, 1) == 0, advantage, -advantage)
+    pair = lax.shift_right_logical(slot, 1)
+    margins = beta_scale * jnp.sum(jnp.where(pair == lane, signed, 0.0), axis=0, keepdims=True)
+    softplus = jnp.maximum(-margins, 0.0) + jnp.log1p(jnp.exp(-jnp.abs(margins)))
+    n_pairs = seqs // 2
+    loss = jnp.sum(jnp.where(lane[:1] < n_pairs, softplus, 0.0), axis=1, keepdims=True) / n_pairs
+    out_ref[0:1, :] = own
+    out_ref[1:2, :] = margins
+    out_ref[2:3, :] = jnp.broadcast_to(loss, margins.shape)
+
+
+def fused(hidden, weight, targets, slot, prompt_len, ref_means):
+    n_tok = lax.axis_size("tok")
+    n_dev = n_tok * lax.axis_size("voc")
+    rows = hidden.shape[0]
+    cols, depth = weight.shape
+    tile = plan_rows(cols)
+    n_z = n_tok // 2
+    whole = pl.BlockSpec(memory_space=pltpu.VMEM)
+    wide = pl.BlockSpec(memory_space=pl.ANY)
+    scalars = pl.BlockSpec(memory_space=pltpu.SMEM)
+    ring = 4
+    copies = 10 * n_z
+    out = pl.pallas_call(
+        functools.partial(fused_kernel, n_tok, n_dev, tile),
+        out_shape=jax.ShapeDtypeStruct((3, rows), jnp.float32),
+        in_specs=[wide, wide, whole, scalars, scalars, scalars],
+        out_specs=whole,
+        scratch_shapes=[
+            pltpu.VMEM((rows * n_tok, depth), hidden.dtype),
+            pltpu.VMEM((ring, 2 * tile, depth), weight.dtype),
+            pltpu.VMEM((tile, 4 * rows), jnp.float32),
+            pltpu.VMEM((tile, 4 * rows), jnp.float32),
+            pltpu.VMEM((SUBS, 4 * rows), jnp.float32),
+            pltpu.VMEM((SUBS, 4 * rows), jnp.float32),
+            pltpu.VMEM((SUBS, 4 * rows), jnp.float32),
+            pltpu.VMEM((n_dev, n_z, 4, rows), jnp.float32),
+            pltpu.VMEM((n_tok, rows), jnp.float32),
+            pltpu.SemaphoreType.DMA((ring, 2)),
+            pltpu.SemaphoreType.DMA,
+            pltpu.SemaphoreType.DMA((copies,)),
+            pltpu.SemaphoreType.DMA((copies,)),
+            pltpu.SemaphoreType.DMA((2, n_dev)),
+            pltpu.SemaphoreType.DMA((2, n_dev)),
+        ],
+        compiler_params=pltpu.CompilerParams(collective_id=3, has_side_effects=True, vmem_limit_bytes=63 * 1024 * 1024),
+        cost_estimate=pl.CostEstimate(flops=2 * rows * n_tok * depth * cols, bytes_accessed=6 * depth * cols, transcendentals=rows * n_tok * cols),
+    )(hidden, weight, targets.reshape(n_tok, rows), slot, prompt_len, ref_means)
+    return out[0], out[1, : n_tok // 2], out[2, 0]
+
+
 def body(hidden, weight, targets, slot, prompt_len, ref_means):
     vocab_cols = weight.shape[1]
+    n_tok = lax.axis_size("tok")
+    rows, width = hidden.shape
+    if lax.axis_size("voc") == 4 and n_tok == 8 and width % LANES == 0 and rows == LANES and vocab_cols >= 10 * plan_rows(vocab_cols) > 0:
+        return fused(hidden, weight.T, targets, slot, prompt_len, ref_means)
     col_start = (lax.axis_index("voc") * lax.axis_size("tok") + lax.axis_index("tok")) * vocab_cols
     local = targets - col_start
     local = jnp.where((local >= 0) & (local < vocab_cols), local, -(1 << 30))

time: 136 us -> 112 us (0.82)
  Pallas kernels: 127 us -> 108 us
  between operations: 2.49 us -> 0.64 us
  local copies, waits for them, and re-layouts: 5.28 us -> 3.58 us
    pallas_call x3 -> x1, Pallas kernels: 127 us -> 108 us  [fused(): pl.pallas_call(functools.partial(fused_kernel, n_tok, n_dev, tile), out_s...]
    broadcast_in_dim x4 -> x0, local copies, waits for them, and re-layouts: 2.96 us -> none  [the longest x3 1.98 us: exchange_and_finish(): wide = lambda v: jnp.broadcast_to(v[:, None], (seqs, width))]
where the time goes in v1:
time: 112 us
  Pallas kernels  108 us (96%)
  local copies, waits for them, and re-layouts  3.58 us (3%)
    pallas_call x1, Pallas kernels, fused(): pl.pallas_call(functools.partial(fused_kernel, n_tok, n_dev, tile), out_s...  108 us
    squeeze x2, local copies, waits for them, and re-layouts, fused(): return (out[0], out[1, :n_tok // 2], out[2, 0])  2.39 us

profile of v1, /device:TPU:0, one launch (start us, length us, event | category | flops | bytes accessed | tf_op | source)
XLA Modules:
  0.0 111.8 jit_solution(16006151959852333662)
XLA Ops:
  0.6 107.6 %shard_map.85 = f32[3,128]{1,0:T(4,128)} custom-call(bf16[128,896]{1,0:T(8,128)(2,1)} %hidden_ref.1, bf16[8000,3584]{1,0:T(8,128)(2,1)} %bitcast.7, s32[8,128]{1,0:T(8,128)} %bitcast.8, s32[8]{0:T(128)} %slot_ref.1, s32[8]{0:T(128)} %prompt_ref.1, f32[8]{0:T(128)} %ref_ref.1), custom_call_target="tpu_custom_call" | custom-call | flops 58720256000 | bytes 172032000 | tf_op jit(solution)/shard_map/pallas_call | solution.py:611
  108.2 1.2 %slice.11 = f32[1,1]{1,0:T(1,128)} slice(f32[3,128]{1,0:T(4,128)} %shard_map.85), slice={[2:3], [0:1]} | slice | bytes 8 | tf_op jit(solution)/shard_map/slice | solution.py:636
  109.4 1.2 %slice_bitcast_fusion = f32[4]{0:T(128)} fusion(f32[3,128]{1,0:T(4,128)} %shard_map.85), kind=kLoop, calls=%fused_computation | loop fusion | bytes 32 | tf_op jit(solution)/shard_map/squeeze | solution.py:636
  110.6 1.2 %slice_bitcast_fusion.1 = f32[128]{0:T(128)} fusion(f32[3,128]{1,0:T(4,128)} %shard_map.85), kind=kLoop, calls=%fused_computation.1 | loop fusion | bytes 1024 | tf_op jit(solution)/shard_map/squeeze | solution.py:636

commit v2 on v1

--- a/solution.py
+++ b/solution.py
@@ -332,7 +332,7 @@
         for i in range(rows // SUBS):
             x = x_ref[i * SUBS : (i + 1) * SUBS, at]
             sums[i % lanes] = sums[i % lanes] + jnp.exp(x - m_new)
-            hits[i % lanes] = hits[i % lanes] + jnp.where(want == i * SUBS, x, 0.0)
+            hits[i % lanes] = jnp.where(want == i * SUBS, x, hits[i % lanes])
         m_ref[:, at] = m_new
         s_ref[:, at] = functools.reduce(jnp.add, sums)
         t_ref[:, at] = functools.reduce(jnp.add, hits)
@@ -340,8 +340,8 @@
 
 def fused_kernel(
     n_tok, n_dev, tile,
-    hidden_ref, weight_ref, tgt_ref, slot_ref, prompt_ref, ref_ref, out_ref,
-    full_ref, ring_ref, a_ref, b_ref, m_ref, s_ref, t_ref, got_ref, lp_ref,
+    hidden_ref, weight_ref, tgt_ref, slot_ref, prompt_ref, ref_ref, own_ref, margin_ref, loss_ref,
+    full_ref, ring_ref, a_ref, b_ref, c_ref, m_ref, s_ref, t_ref, near_ref, got_ref, lp_ref,
     ring_sem, local_sem, send_sem, recv_sem, stat_send, stat_recv,
 ):
     tok, voc = lax.axis_index("tok"), lax.axis_index("voc")
@@ -376,31 +376,29 @@
 
     keep = pltpu.make_async_copy(hidden_ref, place(0, y, voc), local_sem)
     keep.start()
-    for n in range(slots):
+    for n in range(1):
         for part in range(2):
             load(n, part).start()
 
-    def peer(k):
-        other = lax.rem(me + k, n_dev)
-        return {"tok": lax.rem(other, n_tok), "voc": lax.div(other, n_tok)}
-
+    n_voc = n_dev // n_tok
+    peers = [{"tok": (tok + k) % n_tok, "voc": voc} for k in range(1, n_tok)]
+    peers += [{"tok": tok, "voc": (voc + k) % n_voc} for k in range(1, n_voc)]
     barrier = pltpu.get_barrier_semaphore()
-
-    @pl.loop(1, n_dev)
-    def _(k):
-        pl.semaphore_signal(barrier, inc=1, device_id=peer(k), device_id_type=pl.DeviceIdType.MESH)
-
+    for device in peers:
+        pl.semaphore_signal(barrier, inc=1, device_id=device, device_id_type=pl.DeviceIdType.MESH)
     keep.wait()
-    pl.semaphore_wait(barrier, n_dev - 1)
-
-    Z, X, Y, XH, YH, SZ, SX, SY, SXH, SYH = range(10)
+    pl.semaphore_wait(barrier, len(peers))
+
+    Z, X, Y, XH, YH, SZ, SX, SY, SXH, SYH, XL, YL = range(12)
     sent = []
 
     def copy(kind, o):
         t, v, first, count, device = {
             Z: (y, voc, 0, rows, {"tok": ((z + n_z - o) % n_z) * 2 + y, "voc": voc}),
-            X: (y, voc, 0, rows, to_x),
-            Y: (y, voc, 0, rows, to_y),
+            X: (y, voc, 0, half, to_x),
+            XL: (y, voc, half, half, to_x),
+            Y: (y, voc, half, half, to_y),
+            YL: (y, voc, 0, half, to_y),
             SZ: (y, voc, 0, rows, to_sibling),
             YH: (y, other_x, 0, half, to_y),
             SX: (y, other_x, 0, rows, to_sibling),
@@ -426,8 +424,10 @@
     def arrived(kind, o):
         t, v, first, count = {
             Z: (y, voc, 0, rows),
-            X: (y, other_x, 0, rows),
-            Y: (1 - y, voc, 0, rows),
+            X: (y, other_x, 0, half),
+            XL: (y, other_x, half, half),
+            Y: (1 - y, voc, half, half),
+            YL: (1 - y, voc, 0, half),
             SZ: (y, sibling, 0, rows),
             YH: (1 - y, other_x, 0, half),
             SX: (y, far_x, 0, rows),
@@ -449,15 +449,17 @@
     def spread(o):
         if o:
             arrived(Z, o)
-        for kind in (X, Y, SZ):
+        for kind in (X, Y, XL, YL, SZ):
             send(kind, o)
 
     def forward(o):
         arrived(X, o)
         send(YH, o)
-        send(SX, o)
         arrived(Y, o)
         send(XH, o)
+        arrived(XL, o)
+        send(SX, o)
+        arrived(YL, o)
         send(SY, o)
 
     def finish(o):
@@ -470,21 +472,22 @@
         for kind in (SZ, SX, SY, SYH, SXH):
             arrived(kind, o)
 
-    def stat_copy(k, source, piece):
-        part = got_ref.at[source, pl.ds(piece * 2, 2)]
-        return pltpu.make_async_remote_copy(
-            src_ref=part,
-            dst_ref=part,
-            send_sem=stat_send.at[piece, k],
-            recv_sem=stat_recv.at[piece, k],
-            device_id=peer(k),
-            device_id_type=pl.DeviceIdType.MESH,
-        )
-
-    def tell(piece):
-        @pl.loop(1, n_dev)
-        def _(k):
-            stat_copy(k, me, piece).start()
+    def exchange(box, mine, count, device_of, first):
+        def stat(k, source):
+            return pltpu.make_async_remote_copy(
+                src_ref=box.at[source],
+                dst_ref=box.at[source],
+                send_sem=stat_send.at[first + k],
+                recv_sem=stat_recv.at[first + k],
+                device_id=device_of((mine + k) % count),
+                device_id_type=pl.DeviceIdType.MESH,
+            )
+
+        for k in range(1, count):
+            stat(k, mine).start()
+        for k in range(1, count):
+            stat(k, (mine + count - k) % count).wait_recv()
+        return [stat(k, mine) for k in range(1, count)]
 
     spread(0)
     for o in (1, 3, 2):
@@ -492,6 +495,9 @@
     forward(0)
     finish(0)
     settle(0)
+    for n in range(1, slots):
+        for part in range(2):
+            load(n, part).start()
 
     col_start = me * cols
 
@@ -502,9 +508,10 @@
             for t in range(2):
                 local = tgt_ref[pl.ds(((z + o) % n_z) * 2 + t, 1), :] - col_start
                 wanted.append(jnp.where((local >= 0) & (local < cols), local, -(1 << 30)))
-        x_a, x_b = a_ref.at[:, pl.ds(0, size)], b_ref.at[:, pl.ds(0, size)]
+        blocks = ((a_ref, 0), (b_ref, tile)) if planes == 2 else ((c_ref, 0),)
         m, s, t = (r.at[:, pl.ds(0, size)] for r in (m_ref, s_ref, t_ref))
-        x_b[...] = jnp.full_like(x_b, LOW)
+        for x, _ in blocks:
+            x[...] = jnp.full_like(x, LOW)
         m[...] = jnp.full_like(m, LOW)
         s[...] = jnp.zeros_like(s)
         t[...] = jnp.zeros_like(t)
@@ -524,14 +531,15 @@
             slot = lax.rem(n, slots)
             h = lambda: full_ref[first * 2 * rows : first * 2 * rows + size, :]
             base = i * (2 * tile)
-            x_a[...] = lax.dot_general(ring_ref[slot, :tile, :], h(), NT, preferred_element_type=jnp.float32)
-            fold_tile(x_b, wanted, base - tile, m, s, t)
-            x_b[...] = lax.dot_general(ring_ref[slot, tile:, :], h(), NT, preferred_element_type=jnp.float32)
-            fold_tile(x_a, wanted, base, m, s, t)
+            for x, first_row in blocks:
+                fold_tile(x, wanted, base + first_row - 2 * tile, m, s, t)
+                w = ring_ref[slot, first_row : first_row + x.shape[0], :]
+                x[...] = lax.dot_general(w, h(), NT, preferred_element_type=jnp.float32)
             return carry
 
         lax.fori_loop(0, pairs, step, 0)
-        fold_tile(x_b, wanted, cols - tile, m, s, t)
+        for x, first_row in blocks:
+            fold_tile(x, wanted, cols + first_row - 2 * tile, m, s, t)
         high = m[...]
         top = jnp.max(high, axis=0, keepdims=True)
         total = jnp.sum(s[...] * jnp.exp(high - top), axis=0, keepdims=True)
@@ -540,8 +548,8 @@
         for p in range(planes):
             for q in range(2):
                 at = slice((2 * p + q) * LANES, (2 * p + q + 1) * LANES)
-                got_ref[me, first + p, q : q + 1, :] = lse[:, at]
-                got_ref[me, first + p, 2 + q : 3 + q, :] = hit[:, at]
+                near_ref[voc, first + p, q : q + 1, :] = lse[:, at]
+                near_ref[voc, first + p, 2 + q : 3 + q, :] = hit[:, at]
 
     def act(*calls):
         def run():
@@ -550,32 +558,31 @@
 
         return run
 
-    sweep(0, 0, 1, [(0, act((spread, 1))), (2, act((forward, 1), (spread, 3))), (4, act((finish, 1), (forward, 3), (spread, 2)))])
+    sweep(0, 0, 1, [(0, act((spread, 1))), (2, act((forward, 1), (spread, 3))), (4, act((finish, 1), (spread, 2)))])
     settle(1)
-    sweep(1, 1, 1, [(1, act((finish, 3), (forward, 2))), (3, act((finish, 2)))])
+    sweep(1, 1, 1, [(0, act((forward, 3))), (2, act((finish, 3), (forward, 2))), (4, act((finish, 2)))])
     settle(3)
     settle(2)
-    sweep(2, 2, 2, [(1, act((tell, 0)))])
-    tell(1)
+    sweep(2, 2, 2, [])
+
+    def merge(parts):
+        top = functools.reduce(jnp.maximum, [p[:2] for p in parts])
+        total = functools.reduce(jnp.add, [jnp.exp(p[:2] - top) for p in parts])
+        return top + jnp.log(total), functools.reduce(jnp.add, [p[2:] for p in parts])
+
+    pending = exchange(near_ref, voc, n_voc, lambda v: {"tok": tok, "voc": v}, 0)
+    for o in range(n_z):
+        lse, hit = merge([near_ref[v, o] for v in range(n_voc)])
+        got_ref[tok, o, :2, :] = lse
+        got_ref[tok, o, 2:, :] = hit
+    pending += exchange(got_ref, tok, n_tok, lambda t: {"tok": t, "voc": voc}, n_voc)
     for kind, o in sent:
         copy(kind, o).wait_send()
-
-    @pl.loop(1, n_dev)
-    def _(k):
-        for piece in range(2):
-            stat_copy(k, lax.rem(me + n_dev - k, n_dev), piece).wait_recv()
-
-    @pl.loop(1, n_dev)
-    def _(k):
-        for piece in range(2):
-            stat_copy(k, me, piece).wait_send()
-
+    for stat in pending:
+        stat.wait_send()
     for g in range(n_z):
-        of = lambda k: got_ref[k, (g - (k % n_tok) // 2) % n_z]
-        top = functools.reduce(jnp.maximum, [of(k)[:2] for k in range(n_dev)])
-        total = functools.reduce(jnp.add, [jnp.exp(of(k)[:2] - top) for k in range(n_dev)])
-        hit = functools.reduce(jnp.add, [of(k)[2:] for k in range(n_dev)])
-        lp_ref[2 * g : 2 * g + 2, :] = hit - (top + jnp.log(total))
+        lse, hit = merge([got_ref[k, (g - k // 2) % n_z] for k in range(n_tok)])
+        lp_ref[2 * g : 2 * g + 2, :] = hit - lse
     token_lp = lp_ref[...]
     seqs, length = token_lp.shape
     row = lax.broadcasted_iota(jnp.int32, (seqs, length), 0)
@@ -591,9 +598,9 @@
     softplus = jnp.maximum(-margins, 0.0) + jnp.log1p(jnp.exp(-jnp.abs(margins)))
     n_pairs = seqs // 2
     loss = jnp.sum(jnp.where(lane[:1] < n_pairs, softplus, 0.0), axis=1, keepdims=True) / n_pairs
-    out_ref[0:1, :] = own
-    out_ref[1:2, :] = margins
-    out_ref[2:3, :] = jnp.broadcast_to(loss, margins.shape)
+    own_ref[...] = own
+    margin_ref[...] = margins
+    loss_ref[...] = jnp.broadcast_to(loss, margins.shape)
 
 
 def fused(hidden, weight, targets, slot, prompt_len, ref_means):
@@ -607,33 +614,36 @@
     wide = pl.BlockSpec(memory_space=pl.ANY)
     scalars = pl.BlockSpec(memory_space=pltpu.SMEM)
     ring = 4
-    copies = 10 * n_z
-    out = pl.pallas_call(
+    copies = 12 * n_z
+    row = jax.ShapeDtypeStruct((1, rows), jnp.float32)
+    own, margins, loss = pl.pallas_call(
         functools.partial(fused_kernel, n_tok, n_dev, tile),
-        out_shape=jax.ShapeDtypeStruct((3, rows), jnp.float32),
+        out_shape=(row, row, row),
         in_specs=[wide, wide, whole, scalars, scalars, scalars],
-        out_specs=whole,
+        out_specs=(whole, whole, whole),
         scratch_shapes=[
             pltpu.VMEM((rows * n_tok, depth), hidden.dtype),
             pltpu.VMEM((ring, 2 * tile, depth), weight.dtype),
             pltpu.VMEM((tile, 4 * rows), jnp.float32),
             pltpu.VMEM((tile, 4 * rows), jnp.float32),
+            pltpu.VMEM((2 * tile, 2 * rows), jnp.float32),
             pltpu.VMEM((SUBS, 4 * rows), jnp.float32),
             pltpu.VMEM((SUBS, 4 * rows), jnp.float32),
             pltpu.VMEM((SUBS, 4 * rows), jnp.float32),
-            pltpu.VMEM((n_dev, n_z, 4, rows), jnp.float32),
+            pltpu.VMEM((n_dev // n_tok, n_z, 4, rows), jnp.float32),
+            pltpu.VMEM((n_tok, n_z, 4, rows), jnp.float32),
             pltpu.VMEM((n_tok, rows), jnp.float32),
             pltpu.SemaphoreType.DMA((ring, 2)),
             pltpu.SemaphoreType.DMA,
             pltpu.SemaphoreType.DMA((copies,)),
             pltpu.SemaphoreType.DMA((copies,)),
-            pltpu.SemaphoreType.DMA((2, n_dev)),
-            pltpu.SemaphoreType.DMA((2, n_dev)),
+            pltpu.SemaphoreType.DMA((n_dev // n_tok + n_tok,)),
+            pltpu.SemaphoreType.DMA((n_dev // n_tok + n_tok,)),
         ],
         compiler_params=pltpu.CompilerParams(collective_id=3, has_side_effects=True, vmem_limit_bytes=63 * 1024 * 1024),
         cost_estimate=pl.CostEstimate(flops=2 * rows * n_tok * depth * cols, bytes_accessed=6 * depth * cols, transcendentals=rows * n_tok * cols),
     )(hidden, weight, targets.reshape(n_tok, rows), slot, prompt_len, ref_means)
-    return out[0], out[1, : n_tok // 2], out[2, 0]
+    return own.reshape(-1), margins[0, : n_tok // 2], loss[0, 0]
 
 
 def body(hidden, weight, targets, slot, prompt_len, ref_means):

time: 112 us -> 100 us (0.89)
  Pallas kernels: 108 us -> 95.2 us
  between operations: 0.64 us -> 2.4 us
  local copies, waits for them, and re-layouts: 3.58 us -> 2.25 us
    pallas_call x1, Pallas kernels: 108 us -> 95.2 us  [fused(): pl.pallas_call(functools.partial(fused_kernel, n_tok, n_dev, tile), out_s...]
    squeeze x2 -> x1, local copies, waits for them, and re-layouts: 2.39 us -> 1.14 us  [fused(): return (own.reshape(-1), margins[0, :n_tok // 2], loss[0, 0])]
    slice x1 -> x0, local copies, waits for them, and re-layouts: 1.2 us -> none  [fused(): return (out[0], out[1, :n_tok // 2], out[2, 0])]
where the time goes in v2:
time: 100 us; the launch traced here: 99.9 us
  Pallas kernels  95.2 us (95%)
  between operations  2.4 us (2%)
  local copies, waits for them, and re-layouts  2.25 us (2%)
    pallas_call x1, Pallas kernels, fused(): pl.pallas_call(functools.partial(fused_kernel, n_tok, n_dev, tile), out_s...  95.2 us

profile of v2, /device:TPU:0, one launch (start us, length us, event | category | flops | bytes accessed | tf_op | source)
XLA Modules:
  0.0 99.9 jit_solution(9746716993946881327)
XLA Ops:
  0.6 95.2 %shard_map.85 = (f32[1,128]{1,0:T(1,128)}, f32[1,128]{1,0:T(1,128)}, f32[1,128]{1,0:T(1,128)}) custom-call(bf16[128,896]{1,0:T(8,128)(2,1)} %hidden_ref.1, bf16[8000,3584]{1,0:T(8,128)(2,1)} %bitcast.7, s32[8,128]{1,0:T(8,128)} %bitcast.8, s32[8]{0:T(128)} %slot_ref.1, s32[8]{0:T(128)} %prompt_ref.1, f32[8]{0:T(128)} %ref_ref.1), custom_call_target="tpu_custom_call" | custom-call | flops 58720256000 | bytes 172032000 | tf_op jit(solution)/shard_map/pallas_call | solution.py:619
  95.8 1.1 %slice_bitcast_fusion = f32[4]{0:T(128)} fusion(f32[1,128]{1,0:T(1,128)} %get-tuple-element.7), kind=kLoop, calls=%fused_computation | loop fusion | bytes 32 | tf_op jit(solution)/shard_map/squeeze | solution.py:646
  97.0 1.1 %copy.11 = f32[128]{0:T(128)} copy(f32[128]{0:T(128)} %bitcast.10) | data formatting | bytes 1024
